TPU v7x, 32 devices: a whole 2x2x4 slice. The times are simulated.
32 devices in a mesh: clip: 2 (over y), ha: 8 (over z, x), ta: 2 (over core).
Axes of the slice: x: 2, y: 2, z: 4, core: 2. Of those that a mesh axis runs over, the one named last changes fastest.
Arguments:
- latent_tokens: bfloat16 [16, 512, 64], P('clip', ('ha', 'ta')), parts along dimension 0, may hold values from -8 to 8
- w_in: bfloat16 [3, 3, 3, 16, 384], replicated, may hold values from -0.3125 to 0.3125
- b_in: float32 [384], replicated, may hold values from -3 to 3
- gn_gain: float32 [384], replicated, may hold values from 0.1 to 1.9
- gn_shift: float32 [384], replicated, may hold values from -3 to 3
- w_mid: bfloat16 [3, 3, 3, 384, 384], replicated, may hold values from -0.109375 to 0.109375
- b_mid: float32 [384], replicated, may hold values from -3 to 3
Outputs:
- decoded: bfloat16 [16, 16, 128, 384], P(('clip', 'ta'), 'ha'), parts along dimension 0
There are 2 independent parts, one for each index of `clip`. A program takes and returns all parts, laid end to end along the dimension named above; an argument that names none is the same for every part. Nothing has to cross between parts.
All inputs are finite; a program needn't handle non-finite values.
Results may differ from a plain program's by a relative error of at most 0.0054.
Values may be sent and summed in bfloat16 or wider, within the bound.
A program may use at most 64 MiB of HBM per device.

v0:
```python
import jax
import jax.numpy as jnp
from jax import lax
from jax.sharding import PartitionSpec as P

GROUPS = 32
H_DEV = 2
W = 128


eps = 1e-06


def passed_along(value, axis, by):
    devices = lax.axis_size(axis)
    pairs = [(i, i + by) for i in range(devices) if 0 <= i + by < devices]
    return lax.ppermute(value, axis, pairs)


def extended_2(value, sides, width):
    for axis, dim in sides:
        devices, length = (lax.axis_size(axis), value.shape[dim])
        up = [(i, (i + 1) % devices) for i in range(devices - 1)]
        down = [(j, i) for i, j in up]
        last = lax.slice_in_dim(value, length - width, length, axis=dim)
        first = lax.slice_in_dim(value, 0, width, axis=dim)
        before = lax.ppermute(last, axis, up)
        after = lax.ppermute(first, axis, down)
        value = jnp.concatenate([before, value, after], axis=dim)
    return value


def unpatch(tokens, rows, cols):
    frames = tokens.shape[0]
    latent_ch = tokens.shape[2] // 4
    blocks = tokens.reshape(frames, rows // 2, cols // 2, 2, 2, latent_ch)
    return blocks.transpose(0, 1, 3, 2, 4, 5).reshape(frames, rows, cols, latent_ch)


def pad_cols(field):
    return jnp.pad(field, ((0, 0), (0, 0), (1, 1), (0, 0)))


def input_conv(padded, w_in, b_in, frames, rows, cols):
    pieces = [
        padded[frame_tap : frame_tap + frames, row_tap : row_tap + rows, col_tap : col_tap + cols]
        for frame_tap in range(3)
        for row_tap in range(3)
        for col_tap in range(3)
    ]
    stacked = jnp.concatenate(pieces, axis=-1).reshape(frames * rows * cols, -1)
    result = jnp.dot(
        stacked, w_in.reshape(stacked.shape[1], -1), preferred_element_type=jnp.float32
    )
    return (result + b_in).reshape(frames, rows, cols, -1)


def middle_conv(padded, w_mid, frames, rows, cols):
    channels = padded.shape[-1]
    total = jnp.zeros((frames * rows * cols, w_mid.shape[-1]), jnp.float32)
    for frame_tap in range(3):
        for row_tap in range(3):
            slab = jnp.concatenate(
                [
                    padded[
                        frame_tap : frame_tap + frames,
                        row_tap : row_tap + rows,
                        col_tap : col_tap + cols,
                    ]
                    for col_tap in range(3)
                ],
                axis=-1,
            ).reshape(frames * rows * cols, 3 * channels)
            total = total + jnp.dot(
                slab,
                w_mid[frame_tap, row_tap].reshape(3 * channels, -1),
                preferred_element_type=jnp.float32,
            )
    return total.reshape(frames, rows, cols, -1)


def group_totals(field):
    grouped = field.reshape(-1, GROUPS, field.shape[-1] // GROUPS)
    return jnp.sum(grouped, axis=(0, 2))


def normalize(hidden, mean, var, gn_gain, gn_shift):
    members = hidden.shape[-1] // GROUPS
    mean_chan = jnp.repeat(mean, members)
    scale_chan = jnp.repeat(lax.rsqrt(var + eps), members)
    scaled = (hidden.astype(jnp.float32) - mean_chan) * scale_chan * gn_gain + gn_shift
    return jax.nn.silu(scaled).astype(jnp.bfloat16)


def body(latent_tokens, w_in, b_in, gn_gain, gn_shift, w_mid, b_mid):
    rows = H_DEV
    cols = W
    moved = lax.all_to_all(latent_tokens, "ta", split_axis=0, concat_axis=1, tiled=True)
    latent = unpatch(moved, rows, cols)
    frames = latent.shape[0]
    earlier = passed_along(latent, "ta", 1)
    extended = jnp.concatenate([earlier, latent], axis=0)
    framed = extended_2(extended, (("ha", 1),), 2)
    wide_hidden = input_conv(pad_cols(framed), w_in, b_in, frames + 2, rows + 2, cols).astype(
        jnp.bfloat16
    )
    hidden = wide_hidden[2:, 1 : rows + 1]
    values = lax.optimization_barrier(hidden).astype(jnp.float32)
    members = values.shape[-1] // GROUPS
    count = float(lax.axis_size("ha") * lax.axis_size("ta") * frames * rows * cols * members)
    mean = lax.psum(group_totals(values), ("ha", "ta")) / count
    centered = values - jnp.repeat(mean, members)
    var = lax.psum(group_totals(centered * centered), ("ha", "ta")) / count
    active = normalize(wide_hidden, mean, var, gn_gain, gn_shift)
    frame_pos = lax.axis_index("ta") * frames + jnp.arange(frames + 2, dtype=jnp.int32) - 2
    row_pos = lax.axis_index("ha") * rows + jnp.arange(rows + 2, dtype=jnp.int32) - 1
    inside = (
        (frame_pos >= 0)[:, None]
        & (row_pos >= 0)[None, :]
        & (row_pos < rows * lax.axis_size("ha"))[None, :]
    )
    padded = jnp.where(inside[:, :, None, None], active, jnp.zeros_like(active))
    branch = middle_conv(pad_cols(padded), w_mid, frames, rows, cols)
    return (values + branch + b_mid).astype(jnp.bfloat16)


def solution(mesh):
    placed = (P("clip", ("ha", "ta"), None), P(), P(), P(), P(), P(), P())
    return jax.shard_map(
        body,
        mesh=mesh,
        in_specs=placed,
        out_specs=P(("clip", "ta"), "ha", None, None),
        check_vma=False,
    )
```

profile of v0, /device:TPU:0, one launch (start us, length us, event | category | flops | bytes accessed | tf_op | source)
XLA Modules:
  0.0 131.4 jit_solution(58256040233946923)
XLA Ops:
  1.0 3.7 %all_to_all.15 = bf16[2,2,4096]{2,1,0:T(2,128)(2,1)S(1)} all-to-all(bf16[2,2,4096]{2,1,0:T(2,128)(2,1)S(1)} %reshape.124), channel_id=1, replica_groups=mesh['clip'=2,'ha'=8,'ta'=2] {'ta'}, dimensions={0} | all-to-all | bytes 65536 | tf_op jit(solution)/shard_map/all_to_all | solution.py:98
  5.3 2.1 %collective-permute-start = (bf16[4,2,128,16]{3,2,1,0:T(8,128)(2,1)S(1)}, bf16[4,2,128,16]{3,2,1,0:T(8,128)(2,1)S(1)}, u32[]{:S(2)}, u32[]{:S(2)}) collective-permute-start(bf16[4,2,128,16]{3,2,1,0:T(8,128)(2,1)S(1)} %bitcast.63), channel_id=1, source_target_pairs={{0,1},{2,3},{4,5},{6,7},{8,9},{10,11},{12,13},{14,15},{16,17},{18,... | collective-permute-start | bytes 98312 | tf_op jit(solution)/shard_map/ppermute | solution.py:17
  7.4 5.7 %fusion.25 = (bf16[1,1,3,384,384]{4,3,2,1,0:T(8,128)(2,1)}, bf16[1,1,3,384,384]{4,3,2,1,0:T(8,128)(2,1)}, bf16[1,1,3,384,384]{4,3,2,1,0:T(8,128)(2,1)}, bf16[1,1...) fusion(bf16[3,3,3,384,384]{4,3,2,1,0:T(8,128)(2,1)} %param.12), kind=kLoop, calls=%fused_computation.94 | loop fusion | bytes 15925248 | tf_op jit(solution)/shard_map/slice | solution.py:76
  13.4 1.3 collective-permute-start.2
  14.7 5.5 %collective-permute-start.1 = (bf16[8,2,128,16]{2,3,1,0:T(8,128)(2,1)S(1)}, bf16[8,2,128,16]{2,3,1,0:T(8,128)(2,1)S(1)}, u32[]{:S(2)}, u32[]{:S(2)}) collective-permute-start(bf16[8,2,128,16]{2,3,1,0:T(8,128)(2,1)S(1)} %pad_maximum_fusion.11), channel_id=1, source_target_pairs={{0,2},{2,4},{4,6},{6,8},{8,10},{10,12},{12,14},{1,3},{3,5},{5,7},{... | collective-permute-start | bytes 196616 | tf_op jit(solution)/shard_map/ppermute | solution.py:27
  20.6 1.6 %collective-permute-done.1 = bf16[8,2,128,16]{2,3,1,0:T(8,128)(2,1)S(1)} collective-permute-done((bf16[8,2,128,16]{2,3,1,0:T(8,128)(2,1)S(1)}, bf16[8,2,128,16]{2,3,1,0:T(8,128)(2,1)S(1)}, u32[]{:S(2)}, u32[]{:S(2)}) %collective-permute-start.1) | collective-permute-done | bytes 65568 | tf_op jit(solution)/shard_map/ppermute | solution.py:27
  24.5 1.0 copy.18
  25.6 3.2 %reshape.112 = bf16[3072,432]{0,1:T(8,128)(2,1)} reshape(bf16[6,4,128,432]{2,1,0,3:T(4,128)(2,1)S(1)} %copy.18) | data formatting | bytes 5308416 | tf_op jit(solution)/shard_map/reshape | solution.py:51
  28.7 3.6 %add_convert_fusion = bf16[3072,384]{1,0:T(8,128)(2,1)S(1)} fusion(bf16[3072,432]{0,1:T(8,128)(2,1)} %reshape.112, bf16[432,384]{1,0:T(8,128)(2,1)S(1)} %bitcast.49, f32[384]{0:T(512)S(1)} %copy-done.14), kind=kOutput, calls=%fused_computation.1 | convolution fusion | flops 1021575168 | bytes 5346816 | tf_op jit(solution)/shard_map/dot_general | solution.py:52
  32.8 32.9 %psum.14 = f32[32]{0:T(128)S(1)} all-reduce(f32[32]{0:T(128)S(1)} %reduce_sum.25), channel_id=1, replica_groups=mesh['clip'=2,'ha'=8,'ta'=2] {'ha','ta'}, use_global_device_ids=true, to_apply=%region_2.3 | all-reduce | flops 32 | bytes 256 | tf_op jit(solution)/shard_map/psum | solution.py:111
  66.5 29.7 %psum.15 = f32[32]{0:T(128)S(1)} all-reduce(f32[32]{0:T(128)S(1)} %reduce_sum.37), channel_id=1, replica_groups=mesh['clip'=2,'ha'=8,'ta'=2] {'ha','ta'}, use_global_device_ids=true, to_apply=%region_5.6 | all-reduce | flops 32 | bytes 256 | tf_op jit(solution)/shard_map/psum | solution.py:113
  96.4 1.9 %fusion = bf16[6,4,128,384]{3,2,1,0:T(8,128)(2,1)S(1)} fusion(bf16[6,4,128,384]{3,2,1,0:T(8,128)(2,1)S(1)} %bitcast.53, f32[384]{0:T(512)S(1)} %copy-done.11, f32[384]{0:T(512)S(1)} %copy-done.12, f32[384]{0:T(512)S(1)} %mul.34, f32[384]{0:T(512)S(1)} %sub.26, pred[6,4]{1,0:T(8,128)(4,1)S(1)} %and_and_fusion), kind=kLoop, calls=%fused_computation.5 | loop fusion | flops 12976128 | bytes 4724760 | tf_op jit(solution)/shard_map/jit(_where)/select_n | solution.py:122
  98.3 3.6 %pad_slice_fusion.18 = (bf16[4,2,128,384]{3,2,1,0:T(8,128)(2,1)S(1)}, bf16[4,2,128,384]{3,2,1,0:T(8,128)(2,1)S(1)}, bf16[4,2,128,384]{3,2,1,0:T(8,128)(2,1)S(1)}...) fusion(bf16[6,4,128,384]{3,2,1,0:T(8,128)(2,1)S(1)} %fusion), kind=kLoop, calls=%fused_computation.76 | loop fusion | bytes 13369344 | tf_op jit(solution)/shard_map/slice | solution.py:65
  102.6 3.8 %pad_slice_fusion.19 = (bf16[4,2,128,384]{3,2,1,0:T(8,128)(2,1)S(1)}, bf16[4,2,128,384]{3,2,1,0:T(8,128)(2,1)S(1)}, bf16[4,2,128,384]{3,2,1,0:T(8,128)(2,1)S(1)}...) fusion(bf16[6,4,128,384]{3,2,1,0:T(8,128)(2,1)S(1)} %fusion), kind=kLoop, calls=%fused_computation.77 | loop fusion | bytes 11010048 | tf_op jit(solution)/shard_map/slice | solution.py:65
  107.6 1.4 %fusion.34 = f32[1024,384]{1,0:T(8,128)S(1)} fusion(bf16[1024,1152]{1,0:T(8,128)(2,1)S(1)} %bitcast.55, bf16[1152,384]{1,0:T(8,128)(2,1)S(1)} %bitcast.72), kind=kOutput, calls=%fused_computation.103 | convolution fusion | flops 905969664 | bytes 4816896 | tf_op jit(solution)/shard_map/dot_general | solution.py:74
  110.2 1.4 %fusion.33 = f32[1024,384]{1,0:T(8,128)S(1)} fusion(bf16[1024,1152]{1,0:T(8,128)(2,1)S(1)} %bitcast.56, bf16[1152,384]{1,0:T(8,128)(2,1)S(1)} %bitcast.71), kind=kOutput, calls=%fused_computation.102 | convolution fusion | flops 905969664 | bytes 4816896 | tf_op jit(solution)/shard_map/dot_general | solution.py:74
  112.8 1.4 %fusion.32 = f32[1024,384]{1,0:T(8,128)S(1)} fusion(bf16[1024,1152]{1,0:T(8,128)(2,1)S(1)} %bitcast.57, bf16[1152,384]{1,0:T(8,128)(2,1)S(1)} %bitcast.70), kind=kOutput, calls=%fused_computation.101 | convolution fusion | flops 905969664 | bytes 4816896 | tf_op jit(solution)/shard_map/dot_general | solution.py:74
  115.4 1.4 %fusion.31 = f32[1024,384]{1,0:T(8,128)S(1)} fusion(bf16[1024,1152]{1,0:T(8,128)(2,1)S(1)} %bitcast.58, bf16[1152,384]{1,0:T(8,128)(2,1)S(1)} %bitcast.69), kind=kOutput, calls=%fused_computation.100 | convolution fusion | flops 905969664 | bytes 4816896 | tf_op jit(solution)/shard_map/dot_general | solution.py:74
  118.0 1.4 %fusion.30 = f32[1024,384]{1,0:T(8,128)S(1)} fusion(bf16[1024,1152]{1,0:T(8,128)(2,1)S(1)} %bitcast.59, bf16[1152,384]{1,0:T(8,128)(2,1)S(1)} %bitcast.68), kind=kOutput, calls=%fused_computation.99 | convolution fusion | flops 905969664 | bytes 4816896 | tf_op jit(solution)/shard_map/dot_general | solution.py:74
  120.6 1.4 %fusion.29 = f32[1024,384]{1,0:T(8,128)S(1)} fusion(bf16[1024,1152]{1,0:T(8,128)(2,1)S(1)} %bitcast.60, bf16[1152,384]{1,0:T(8,128)(2,1)S(1)} %bitcast.67), kind=kOutput, calls=%fused_computation.98 | convolution fusion | flops 905969664 | bytes 4816896 | tf_op jit(solution)/shard_map/dot_general | solution.py:74
  123.2 1.4 %fusion.27 = f32[1024,384]{1,0:T(8,128)S(1)} fusion(bf16[1024,1152]{1,0:T(8,128)(2,1)S(1)} %bitcast.61, bf16[1152,384]{1,0:T(8,128)(2,1)S(1)} %bitcast.66), kind=kOutput, calls=%fused_computation.96 | convolution fusion | flops 905969664 | bytes 4816896 | tf_op jit(solution)/shard_map/dot_general | solution.py:74
  125.8 1.4 %fusion.28 = f32[1024,384]{1,0:T(8,128)S(1)} fusion(bf16[1024,1152]{1,0:T(8,128)(2,1)S(1)} %bitcast.62, bf16[1152,384]{1,0:T(8,128)(2,1)S(1)} %bitcast.65), kind=kOutput, calls=%fused_computation.97 | convolution fusion | flops 905969664 | bytes 4816896 | tf_op jit(solution)/shard_map/dot_general | solution.py:74
  128.5 1.7 %add_add_fusion = f32[1024,384]{1,0:T(8,128)S(1)} fusion(f32[1024,384]{1,0:T(8,128)S(1)} %fusion.34, f32[1024,384]{1,0:T(8,128)S(1)} %fusion.33, f32[1024,384]{1,0:T(8,128)S(1)} %fusion.32, f32[1024,384]{1,0:T(8,128)S(1)} %fusion.31, f32[1024,384]{1,0:T(8,128)S(1)} %fusion.30, f32[1024,384]{1,0:T(8,128)S(1)} %fusion.29, f32[1024,384]{1,0:T(8,128)S(1)} %fusion.27, ...), kind=kOutput, calls=%fused_computation.19 | convolution fusion | flops 909115392 | bytes 17399808 | tf_op jit(solution)/shard_map/dot_general | solution.py:74
  130.2 1.1 fusion.4
  (95 shorter events, 16.7 us)
Async XLA Ops:
  0.0 28.7 %copy-start = (bf16[3,3,3,16,384]{4,3,2,1,0:T(8,128)(2,1)S(1)}, bf16[3,3,3,16,384]{4,3,2,1,0:T(8,128)(2,1)}, u32[]{:S(2)}) copy-start(bf16[3,3,3,16,384]{4,3,2,1,0:T(8,128)(2,1)} %param.8) | copy-start | bytes 995332
  5.3 8.0 %collective-permute-start = (bf16[4,2,128,16]{3,2,1,0:T(8,128)(2,1)S(1)}, bf16[4,2,128,16]{3,2,1,0:T(8,128)(2,1)S(1)}, u32[]{:S(2)}, u32[]{:S(2)}) collective-permute-start(bf16[4,2,128,16]{3,2,1,0:T(8,128)(2,1)S(1)} %bitcast.63), channel_id=1, source_target_pairs={{0,1},{2,3},{4,5},{6,7},{8,9},{10,11},{12,13},{14,15},{16,17},{18,... | collective-permute-start | bytes 98312 | tf_op jit(solution)/shard_map/ppermute | solution.py:17
  13.4 7.1 %collective-permute-start.2 = (bf16[8,2,128,16]{2,3,1,0:T(8,128)(2,1)S(1)}, bf16[8,2,128,16]{2,3,1,0:T(8,128)(2,1)S(1)}, u32[]{:S(2)}, u32[]{:S(2)}) collective-permute-start(bf16[8,2,128,16]{2,3,1,0:T(8,128)(2,1)S(1)} %pad_maximum_fusion.11), channel_id=1, source_target_pairs={{2,0},{4,2},{6,4},{8,6},{10,8},{12,10},{14,12},{3,1},{5,3},{7,5},{... | collective-permute-start | bytes 196616 | tf_op jit(solution)/shard_map/ppermute | solution.py:28
  14.7 7.4 %collective-permute-start.1 = (bf16[8,2,128,16]{2,3,1,0:T(8,128)(2,1)S(1)}, bf16[8,2,128,16]{2,3,1,0:T(8,128)(2,1)S(1)}, u32[]{:S(2)}, u32[]{:S(2)}) collective-permute-start(bf16[8,2,128,16]{2,3,1,0:T(8,128)(2,1)S(1)} %pad_maximum_fusion.11), channel_id=1, source_target_pairs={{0,2},{2,4},{4,6},{6,8},{8,10},{10,12},{12,14},{1,3},{3,5},{5,7},{... | collective-permute-start | bytes 196616 | tf_op jit(solution)/shard_map/ppermute | solution.py:27
  25.5 3.2 %copy-start.14 = (f32[384]{0:T(512)S(1)}, f32[384]{0:T(512)}, u32[]{:S(2)}) copy-start(f32[384]{0:T(512)} %param.9) | copy-start | bytes 4612
  32.3 64.0 %copy-start.11 = (f32[384]{0:T(512)S(1)}, f32[384]{0:T(512)}, u32[]{:S(2)}) copy-start(f32[384]{0:T(512)} %param.11) | copy-start | bytes 4612
  32.3 64.0 %copy-start.12 = (f32[384]{0:T(512)S(1)}, f32[384]{0:T(512)}, u32[]{:S(2)}) copy-start(f32[384]{0:T(512)} %param.10) | copy-start | bytes 4612
  106.4 1.2 copy-start.10
  109.0 1.2 copy-start.9
  111.6 1.2 copy-start.8
  114.2 1.2 copy-start.7
  116.8 1.2 copy-start.6
  119.5 1.2 copy-start.5
  122.1 1.2 copy-start.4
  124.7 1.2 copy-start.3
  127.3 1.2 copy-start.2
  128.5 1.8 %copy-start.13 = (f32[384]{0:T(512)S(1)}, f32[384]{0:T(512)}, u32[]{:S(2)}) copy-start(f32[384]{0:T(512)} %param.13) | copy-start | bytes 4612
  128.5 2.9 %copy-start.1 = (bf16[3,3,3,16,384]{4,3,2,1,0:T(8,128)(2,1)S(1)}, bf16[3,3,3,16,384]{4,3,2,1,0:T(8,128)(2,1)}, u32[]{:S(2)}) copy-start(bf16[3,3,3,16,384]{4,3,2,1,0:T(8,128)(2,1)} %param.8) | copy-start | bytes 995332
where the time goes:
time: 132 us; the launch traced here: 131 us
  blocking collectives  66.4 us (50%)
  local copies, waits for them, and re-layouts  30.3 us (23%)
  matrix products  16.8 us (13%)
  starting transfers between devices  8.88 us (7%)
  other arithmetic  6.55 us (5%)
  waiting for transfers between devices  1.81 us (1%)
    psum x1, blocking collectives, body(): mean = lax.psum(group_totals(values), ('ha', 'ta')) / count  32.9 us
    psum x1, blocking collectives, body(): var = lax.psum(group_totals(centered * centered), ('ha', 'ta')) / count  29.7 us
    dot_general x9, matrix products, middle_conv(): jnp.dot(slab, w_mid[frame_tap, row_tap].reshape(3 * channels, -1), prefer...  13.2 us
    unnamed x58, local copies, waits for them, and re-layouts  10.8 us
    slice x3, local copies, waits for them, and re-layouts, middle_conv(): padded[frame_tap:frame_tap + frames, row_tap:row_tap + rows, col_tap:col_...  8.12 us
    slice x1, local copies, waits for them, and re-layouts, middle_conv(): w_mid[frame_tap, row_tap].reshape(3 * channels, -1)  5.75 us
    ppermute x1, starting transfers between devices, extended_2(): before = lax.ppermute(last, axis, up)  5.5 us
    all_to_all x1, blocking collectives, body(): lax.all_to_all(latent_tokens, 'ta', split_axis=0, concat_axis=1, tiled=True)  3.75 us
  transfers between devices with their start and end apart: 3, of which 2 were waited for; matrix products, arithmetic and copies ran while one was open for 5% of the time, Pallas kernels for 0%

commit v1 on v0

v1 whole, which is shorter than its diff:
```python
import functools

import jax
import jax.numpy as jnp
from jax import lax
from jax.experimental import pallas as pl
from jax.experimental.pallas import tpu as pltpu
from jax.sharding import PartitionSpec as P

GROUPS = 32
EPS = 1e-06
F32 = jnp.float32
BF16 = jnp.bfloat16
MESH = pl.DeviceIdType.MESH
LANES = 128


def split_dot(rows, ones):
    first = rows.astype(BF16).astype(F32)
    rest = rows - first
    second = rest.astype(BF16).astype(F32)
    third = rest - second
    stacked = jnp.concatenate([first, second, third, jnp.zeros_like(first)] * 2, axis=0)
    keep = lax.broadcasted_iota(jnp.int32, stacked.shape, 0) < 3
    stacked = jnp.where(keep, stacked, 0.0).astype(BF16)
    return jnp.sum(jnp.dot(stacked, ones, preferred_element_type=F32), axis=0, keepdims=True)


def group_of(index, members):
    return jnp.floor((index.astype(F32) + 0.5) * (1.0 / members))


def kernel(
    n_ha, n_ta, tok, w_in, b_in, gain, shift, w_mid, b_mid, out,
    pk, rx, wexp, patch, hid, act, acc, stage, wv, stat, gath, sums, spread,
    w_sem, tx_a, tx_b, rx_a, rx_b, st_tx, st_rx,
):
    h = lax.axis_index("ha")
    t = lax.axis_index("ta")
    n = n_ha * n_ta
    me = h * n_ta + t
    frames, half, width = tok.shape
    fr = frames // n_ta
    ch = b_in.shape[-1]
    members = ch // GROUPS
    cj = half * n_ta
    zc = width // 4
    ext = fr + 2

    for k in range(9):
        pltpu.make_async_copy(w_mid.at[k], wv.at[k], w_sem.at[k]).start()

    packed = jnp.concatenate([tok[:, : half // 2, :], tok[:, half // 2 :, :]], axis=-1)
    pk[...] = packed
    rx[...] = jnp.zeros_like(rx)
    rx[1, t, pl.ds(fr * (1 - t), fr)] = packed[:fr]

    @pl.when(t == 1)
    def _():
        rx[1, 1, fr:] = packed[fr:]

    barrier = pltpu.get_barrier_semaphore()

    def greet(k, c):
        peer = lax.rem(me + k, n)
        pl.semaphore_signal(
            barrier, inc=1, device_id={"ha": peer // n_ta, "ta": peer % n_ta}, device_id_type=MESH
        )
        return c

    lax.fori_loop(1, n, greet, 0)

    zero = jnp.zeros((zc, ch), BF16)
    for p in range(3):
        for block in range(4):
            for a1 in range(2):
                for b1 in range(2):
                    dy = (-1 if a1 else 2) if block >= 2 else a1
                    dx = (-1 if b1 else 2) if block % 2 else b1
                    row = p * 16 * zc + block * 4 * zc + (2 * a1 + b1) * zc
                    for a in range(2):
                        for b in range(2):
                            q, r = dy - a + 1, dx - b + 1
                            inside = 0 <= q <= 2 and 0 <= r <= 2
                            piece = w_in[3 * p + q, r * zc : (r + 1) * zc, :] if inside else zero
                            col = (2 * a + b) * ch
                            wexp[row : row + zc, col : col + ch] = piece
    chan = lax.broadcasted_iota(jnp.int32, (ch, ch + LANES), 0)
    lane = lax.broadcasted_iota(jnp.int32, (ch, ch + LANES), 1)
    target = jnp.where(lane < ch, group_of(lane, members), (lane - ch).astype(F32))
    sums[...] = jnp.where(group_of(chan, members) == target, 1.0, 0.0).astype(BF16)
    chan = lax.broadcasted_iota(jnp.int32, (LANES, ch), 1)
    lane = lax.broadcasted_iota(jnp.int32, (LANES, ch), 0)
    spread[...] = jnp.where(group_of(chan, members) == lane.astype(F32), 1.0, 0.0).astype(BF16)

    pl.semaphore_wait(barrier, n - 1)

    partners = [(0, 1), (1, 0), (-1, 0), (1, 1), (-1, 1)]

    def copies(s):
        dh, dt = partners[s]
        other = (t + dt) % n_ta
        to = {"ha": h + dh, "ta": other}
        first = pltpu.make_async_remote_copy(
            src_ref=pk.at[pl.ds(0, fr)],
            dst_ref=rx.at[1 - dh, t, pl.ds(fr * (1 - other), fr)],
            send_sem=tx_a.at[s], recv_sem=rx_a.at[s], device_id=to, device_id_type=MESH,
        )
        second = pltpu.make_async_remote_copy(
            src_ref=pk.at[pl.ds(fr, fr)],
            dst_ref=rx.at[1 - dh, t, pl.ds(fr, fr)],
            send_sem=tx_b.at[s], recv_sem=rx_b.at[s], device_id=to, device_id_type=MESH,
        )
        return first, second, other

    def exists(s, sign):
        dh = partners[s][0] * sign
        return jnp.logical_and(h + dh >= 0, h + dh < n_ha)

    for s in range(5):

        @pl.when(exists(s, 1))
        def _(s=s):
            first, second, other = copies(s)
            first.start()

            @pl.when(other == 1)
            def _():
                second.start()

    for s in range(5):

        @pl.when(exists(s, -1))
        def _(s=s):
            first, second, _ = copies(s)
            first.wait_recv()

            @pl.when(t == 1)
            def _():
                second.wait_recv()

    rows = frames * cj
    j = lax.broadcasted_iota(jnp.int32, (rows, width), 0) & (cj - 1)
    lane = lax.broadcasted_iota(jnp.int32, (rows, width), 1)
    upper_b = (lane & zc) != 0
    wide = []
    for i in range(3):
        parts = []
        for side in range(n_ta):
            held = rx[i, side].astype(F32)
            parts += [held[:, :, :width], held[:, :, width:]]
        field = jnp.concatenate(parts, axis=1).reshape(rows, width)
        left = jnp.where(j == 0, 0.0, pltpu.roll(field, 1, 0))
        right = jnp.where(j == cj - 1, 0.0, pltpu.roll(field, rows - 1, 0))
        wide.append(jnp.concatenate([field, jnp.where(upper_b, left, right)], axis=-1))
    lane = lax.broadcasted_iota(jnp.int32, (rows, 2 * width), 1)
    upper_a = (lane & (2 * zc)) != 0
    nothing = jnp.zeros_like(wide[0])
    for i in range(3):
        above = wide[i - 1] if i > 0 else nothing
        below = wide[i + 1] if i < 2 else nothing
        crossed = jnp.where(upper_a, above, below)
        patch[i, :, : 2 * width] = wide[i].astype(BF16)
        patch[i, :, 2 * width :] = crossed.astype(BF16)

    def conv(i, lo, count, col0, ncol):
        lhs = jnp.concatenate(
            [patch[i, (lo + p) * cj : (lo + p + count) * cj, :] for p in range(3)], axis=-1
        )
        got = jnp.dot(lhs, wexp[:, col0 : col0 + ncol], preferred_element_type=F32)
        results = []
        for piece in range(ncol // ch):
            value = (got[:, piece * ch : (piece + 1) * ch] + b_in[...]).astype(BF16)
            results.append(value)
        return results

    own = conv(1, 2, fr, 0, 4 * ch)
    total = jnp.zeros((1, ch), F32)
    for ab in range(4):
        hid[2:, 1 + ab // 2, ab % 2] = own[ab].reshape(fr, cj, ch)
        total = total + jnp.sum(own[ab].astype(F32), axis=0, keepdims=True)
    cells = 4 * fr * cj
    chan_mean = total * (1.0 / cells)
    squares = jnp.zeros((1, ch), F32)
    for ab in range(4):
        value = hid[2:, 1 + ab // 2, ab % 2].reshape(fr * cj, ch).astype(F32) - chan_mean
        squares = squares + jnp.sum(value * value, axis=0, keepdims=True)
    grouped = split_dot(chan_mean, sums[...]) * (1.0 / members)
    apart = chan_mean - grouped[:, :ch]
    local_m2 = split_dot(squares + cells * apart * apart, sums[:, ch:])
    stat[...] = jnp.concatenate([grouped[:, ch:], local_m2], axis=0)
    gath[me] = stat[...]

    def share(k, c):
        peer = lax.rem(me + k, n)
        pltpu.make_async_remote_copy(
            src_ref=stat, dst_ref=gath.at[me], send_sem=st_tx, recv_sem=st_rx,
            device_id={"ha": peer // n_ta, "ta": peer % n_ta}, device_id_type=MESH,
        ).start()
        return c

    lax.fori_loop(1, n, share, 0)

    early = conv(1, 0, 2, 0, 4 * ch)
    for ab in range(4):
        hid[:2, 1 + ab // 2, ab % 2] = early[ab].reshape(2, cj, ch)
    over = conv(0, 0, ext, 2 * ch, 2 * ch)
    under = conv(2, 0, ext, 0, 2 * ch)
    for b in range(2):
        hid[:, 0, b] = over[b].reshape(ext, cj, ch)
        hid[:, 3, b] = under[b].reshape(ext, cj, ch)

    others = gath.at[pl.ds(0, n - 1)]
    pltpu.make_async_copy(others, others, st_rx).wait()
    pltpu.make_async_copy(others, others, st_tx).wait()
    for s in range(5):

        @pl.when(exists(s, 1))
        def _(s=s):
            first, second, other = copies(s)
            first.wait_send()

            @pl.when(other == 1)
            def _():
                second.wait_send()

    every = gath[...]
    means = every[:, 0:1, :]
    mean = jnp.sum(means, axis=0) * (1.0 / n)
    gap = means - mean[None]
    count = float(cells * members)
    m2 = jnp.sum(every[:, 1:2, :], axis=0) + count * jnp.sum(gap * gap, axis=0)
    mean_c = split_dot(mean, spread[...])
    var_c = split_dot(m2 * (1.0 / (count * n)), spread[...])
    scale_c = lax.rsqrt(var_c + EPS) * gain[...]

    j = lax.broadcasted_iota(jnp.int32, (cj, ch), 0)

    def activate(k, c):
        lf, y = k // 4, k % 4
        good = jnp.logical_and(
            t * fr + lf >= 2, jnp.logical_and(h * 2 + y >= 1, h * 2 + y < 2 * n_ha + 1)
        )
        live = jnp.where(good, 0.5, 0.0)
        pair = []
        for b in range(2):
            v = (hid[lf, y, b].astype(F32) - mean_c) * scale_c + shift[...]
            pair.append((v * live) * (1.0 + jnp.tanh(0.5 * v)))
        even, odd = pair
        odd_left = jnp.where(j == 0, 0.0, pltpu.roll(odd, 1, 0)).astype(BF16)
        even_right = jnp.where(j == cj - 1, 0.0, pltpu.roll(even, cj - 1, 0)).astype(BF16)
        even, odd = even.astype(BF16), odd.astype(BF16)
        for b, pieces in enumerate(((odd_left, even, odd), (even, odd, even_right))):
            for r in range(3):
                act[lf, y, b * cj : (b + 1) * cj, r * ch : (r + 1) * ch] = pieces[r]
        return c

    lax.fori_loop(0, ext * 4, activate, 0)

    acc[...] = jnp.zeros_like(acc)

    def tap(k, c):
        pltpu.make_async_copy(w_mid.at[k], wv.at[k], w_sem.at[k]).wait()
        lhs = act[pl.ds(k // 3, fr), pl.ds(k % 3, 2)].reshape(fr * 4 * cj, 3 * ch)
        acc[...] += jnp.dot(lhs, wv[k], preferred_element_type=F32)
        return c

    lax.fori_loop(0, 9, tap, 0)

    for f in range(fr):
        for y in range(2):
            base = (f * 2 + y) * 2 * cj
            for b in range(2):
                value = acc[base + b * cj : base + (b + 1) * cj, :] + b_mid[...]
                value = value + hid[f + 2, y + 1, b].astype(F32)
                for piece in range(ch // LANES):
                    cols = slice(piece * LANES, (piece + 1) * LANES)
                    stage[f * 2 + y, piece, pl.ds(b, cj, 2), :] = value[:, cols]
            for piece in range(ch // LANES):
                cols = slice(piece * LANES, (piece + 1) * LANES)
                out[f, y, :, cols] = stage[f * 2 + y, piece].astype(BF16)


def body(n_ha, n_ta, latent_tokens, w_in, b_in, gn_gain, gn_shift, w_mid, b_mid):
    frames, half, width = latent_tokens.shape
    ch = b_in.shape[0]
    zc = width // 4
    fr, cj, n = frames // n_ta, half * n_ta, n_ha * n_ta
    vm = pl.BlockSpec(memory_space=pltpu.VMEM)
    row = lambda v: v.reshape(1, ch)
    return pl.pallas_call(
        functools.partial(kernel, n_ha, n_ta),
        out_shape=jax.ShapeDtypeStruct((fr, 2, 2 * cj, ch), BF16),
        in_specs=[vm, vm, vm, vm, vm, pl.BlockSpec(memory_space=pl.ANY), vm],
        out_specs=vm,
        scratch_shapes=[
            pltpu.VMEM((frames, half // 2, 2 * width), BF16),
            pltpu.VMEM((3, n_ta, frames, half // 2, 2 * width), BF16),
            pltpu.VMEM((48 * zc, 4 * ch), BF16),
            pltpu.VMEM((3, frames * cj, 4 * width), BF16),
            pltpu.VMEM((fr + 2, 4, 2, cj, ch), BF16),
            pltpu.VMEM((fr + 2, 4, 2 * cj, 3 * ch), BF16),
            pltpu.VMEM((fr * 4 * cj, ch), F32),
            pltpu.VMEM((fr * 2, ch // LANES, 2 * cj, LANES), F32),
            pltpu.VMEM((9, 3 * ch, ch), BF16),
            pltpu.VMEM((2, LANES), F32),
            pltpu.VMEM((n, 2, LANES), F32),
            pltpu.VMEM((ch, ch + LANES), BF16),
            pltpu.VMEM((LANES, ch), BF16),
            pltpu.SemaphoreType.DMA((9,)),
            pltpu.SemaphoreType.DMA((5,)),
            pltpu.SemaphoreType.DMA((5,)),
            pltpu.SemaphoreType.DMA((5,)),
            pltpu.SemaphoreType.DMA((5,)),
            pltpu.SemaphoreType.DMA,
            pltpu.SemaphoreType.DMA,
        ],
        compiler_params=pltpu.CompilerParams(
            collective_id=0, has_side_effects=True, vmem_limit_bytes=60 * 1024 * 1024
        ),
    )(
        latent_tokens, w_in.reshape(9, 3 * zc, ch), row(b_in), row(gn_gain), row(gn_shift),
        w_mid.reshape(9, 3 * ch, ch), row(b_mid),
    )


def solution(mesh):
    placed = (P("clip", ("ha", "ta"), None), P(), P(), P(), P(), P(), P())
    return jax.shard_map(
        functools.partial(body, mesh.shape["ha"], mesh.shape["ta"]),
        mesh=mesh,
        in_specs=placed,
        out_specs=P(("clip", "ta"), "ha", None, None),
        check_vma=False,
    )
```

time: 132 us -> 39.7 us (0.30)
  blocking collectives: 66.4 us -> 0 us
  Pallas kernels: 0 us -> 32.3 us
  local copies, waits for them, and re-layouts: 30.3 us -> 7.11 us
  matrix products: 16.8 us -> 0 us
  starting transfers between devices: 8.88 us -> 0 us
  other arithmetic: 6.55 us -> 0 us
  waiting for transfers between devices: 1.81 us -> 0 us
    psum x2 -> x0, blocking collectives: 62.6 us -> none  [the longest x1 32.9 us: body(): mean = lax.psum(group_totals(values), ('ha', 'ta')) / count]
    pallas_call x0 -> x1, Pallas kernels: none -> 32.3 us  [body(): pl.pallas_call(functools.partial(kernel, n_ha, n_ta), out_shape=jax.Shape...]
    dot_general x10 -> x0, matrix products: 16.8 us -> none  [the longest x9 13.2 us: middle_conv(): jnp.dot(slab, w_mid[frame_tap, row_tap].reshape(3 * channels, -1), prefer...]
    slice x5 -> x0, local copies, waits for them, and re-layouts: 14 us -> none  [the longest x3 8.12 us: middle_conv(): padded[frame_tap:frame_tap + frames, row_tap:row_tap + rows, col_tap:col_...]
    ppermute x3 -> x0, starting transfers between devices: 8.88 us -> none  [the longest x1 5.5 us: extended_2(): before = lax.ppermute(last, axis, up)]
    unnamed x58 -> x1, local copies, waits for them, and re-layouts: 10.8 us -> 2.09 us
    all_to_all x1 -> x0, blocking collectives: 3.75 us -> none  [body(): lax.all_to_all(latent_tokens, 'ta', split_axis=0, concat_axis=1, tiled=True)]
    concatenate x12 -> x0, other arithmetic: 2.74 us -> none  [the longest x9 2.68 us: middle_conv(): jnp.concatenate([padded[frame_tap:frame_tap + frames, row_tap:row_tap + r...]
  transfers between devices with their start and end apart: 3 -> 0, of which waited for: 2 -> 0; matrix products, arithmetic and copies ran while one was open for 5% -> 0% of each run, Pallas kernels for 0% -> 0%
where the time goes in v1:
time: 39.7 us; the launch traced here: 39.4 us
  Pallas kernels  32.3 us (81%)
  local copies, waits for them, and re-layouts  7.11 us (18%)
    pallas_call x1, Pallas kernels, body(): pl.pallas_call(functools.partial(kernel, n_ha, n_ta), out_shape=jax.Shape...  32.3 us
    reshape x4, local copies, waits for them, and re-layouts, body(): row = lambda v: v.reshape(1, ch)  5.02 us
    unnamed x1, local copies, waits for them, and re-layouts  2.09 us

profile of v1, /device:TPU:0, one launch (start us, length us, event | category | flops | bytes accessed | tf_op | source)
XLA Modules:
  0.0 39.4 jit_solution(6514331699817143608)
XLA Ops:
  0.0 1.2 %reshape.19.b_in = f32[1,384]{1,0:T(1,128)} reshape(f32[384]{0:T(512)} %param.9) | data formatting | bytes 3072 | tf_op jit(solution)/shard_map/reshape | solution.py:290
  1.2 1.3 %reshape.20.gain = f32[1,384]{1,0:T(1,128)} reshape(f32[384]{0:T(512)} %param.10) | data formatting | bytes 3072 | tf_op jit(solution)/shard_map/reshape | solution.py:290
  2.5 1.3 %reshape.21.shift = f32[1,384]{1,0:T(1,128)} reshape(f32[384]{0:T(512)} %param.11) | data formatting | bytes 3072 | tf_op jit(solution)/shard_map/reshape | solution.py:290
  3.8 1.2 %reshape.23.b_mid = f32[1,384]{1,0:T(1,128)} reshape(f32[384]{0:T(512)} %param.13) | data formatting | bytes 3072 | tf_op jit(solution)/shard_map/reshape | solution.py:290
  5.0 32.3 %shard_map.73 = bf16[4,2,128,384]{3,2,1,0:T(8,128)(2,1)} custom-call(bf16[8,32,64]{2,1,0:T(8,128)(2,1)} %tok.1, bf16[9,48,384]{2,1,0:T(8,128)(2,1)} %bitcast.3, f32[1,384]{1,0:T(1,128)} %reshape.19.b_in, f32[1,384]{1,0:T(1,128)} %reshape.20.gain, f32[1,384]{1,0:T(1,128)} %reshape.21.shift, bf16[9,1152,384]{2,1,0:T(8,128)(2,1)} %bitcast.2, ...), custom_call_target="tpu_custom_call" | custom-call | tf_op jit(solution)/shard_map/pallas_call | solution.py:291
  37.3 2.1 %copy.9 = bf16[4,2,128,384]{3,2,1,0:T(8,128)(2,1)} copy(bf16[4,2,128,384]{3,2,1,0:T(8,128)(2,1)} %shard_map.73) | data formatting | bytes 1572864

commit v2 on v1

--- a/solution.py
+++ b/solution.py
@@ -32,7 +32,7 @@
 
 def kernel(
     n_ha, n_ta, tok, w_in, b_in, gain, shift, w_mid, b_mid, out,
-    pk, rx, wexp, patch, hid, act, acc, stage, wv, stat, gath, sums, spread,
+    pk, rx, wexp, patch, hid, act, stage, wv, stat, gath, sums, spread,
     w_sem, tx_a, tx_b, rx_a, rx_b, st_tx, st_rx,
 ):
     h = lax.axis_index("ha")
@@ -46,6 +46,7 @@
     cj = half * n_ta
     zc = width // 4
     ext = fr + 2
+    b_in_c, gain_c, shift_c, b_mid_c = [v[...].reshape(1, ch) for v in (b_in, gain, shift, b_mid)]
 
     for k in range(9):
         pltpu.make_async_copy(w_mid.at[k], wv.at[k], w_sem.at[k]).start()
@@ -170,7 +171,7 @@
         got = jnp.dot(lhs, wexp[:, col0 : col0 + ncol], preferred_element_type=F32)
         results = []
         for piece in range(ncol // ch):
-            value = (got[:, piece * ch : (piece + 1) * ch] + b_in[...]).astype(BF16)
+            value = (got[:, piece * ch : (piece + 1) * ch] + b_in_c).astype(BF16)
             results.append(value)
         return results
 
@@ -232,53 +233,55 @@
     m2 = jnp.sum(every[:, 1:2, :], axis=0) + count * jnp.sum(gap * gap, axis=0)
     mean_c = split_dot(mean, spread[...])
     var_c = split_dot(m2 * (1.0 / (count * n)), spread[...])
-    scale_c = lax.rsqrt(var_c + EPS) * gain[...]
-
-    j = lax.broadcasted_iota(jnp.int32, (cj, ch), 0)
-
-    def activate(k, c):
-        lf, y = k // 4, k % 4
-        good = jnp.logical_and(
-            t * fr + lf >= 2, jnp.logical_and(h * 2 + y >= 1, h * 2 + y < 2 * n_ha + 1)
-        )
-        live = jnp.where(good, 0.5, 0.0)
-        pair = []
-        for b in range(2):
-            v = (hid[lf, y, b].astype(F32) - mean_c) * scale_c + shift[...]
-            pair.append((v * live) * (1.0 + jnp.tanh(0.5 * v)))
-        even, odd = pair
-        odd_left = jnp.where(j == 0, 0.0, pltpu.roll(odd, 1, 0)).astype(BF16)
-        even_right = jnp.where(j == cj - 1, 0.0, pltpu.roll(even, cj - 1, 0)).astype(BF16)
-        even, odd = even.astype(BF16), odd.astype(BF16)
-        for b, pieces in enumerate(((odd_left, even, odd), (even, odd, even_right))):
-            for r in range(3):
-                act[lf, y, b * cj : (b + 1) * cj, r * ch : (r + 1) * ch] = pieces[r]
-        return c
-
-    lax.fori_loop(0, ext * 4, activate, 0)
-
-    acc[...] = jnp.zeros_like(acc)
-
-    def tap(k, c):
+    scale_c = lax.rsqrt(var_c + EPS) * gain_c
+
+    edge = lax.broadcasted_iota(jnp.int32, (cj, ch), 0)
+
+    def activate(lf):
+        for y in range(4):
+            good = jnp.logical_and(
+                t * fr + lf >= 2, jnp.logical_and(h * 2 + y >= 1, h * 2 + y < 2 * n_ha + 1)
+            )
+            live = jnp.where(good, 0.5, 0.0)
+            for b in range(2):
+                v = (hid[lf, y, b].astype(F32) - mean_c) * scale_c + shift_c
+                v = ((v * live) * (1.0 + jnp.tanh(0.5 * v))).astype(BF16)
+                for q in range(3):
+                    if 0 <= y - q < 2:
+                        act[lf, y - q, b * cj : (b + 1) * cj, q * ch : (q + 1) * ch] = v
+
+    lax.fori_loop(0, ext, lambda lf, c: (activate(lf), c)[1], 0)
+    for k in range(9):
         pltpu.make_async_copy(w_mid.at[k], wv.at[k], w_sem.at[k]).wait()
-        lhs = act[pl.ds(k // 3, fr), pl.ds(k % 3, 2)].reshape(fr * 4 * cj, 3 * ch)
-        acc[...] += jnp.dot(lhs, wv[k], preferred_element_type=F32)
-        return c
-
-    lax.fori_loop(0, 9, tap, 0)
-
-    for f in range(fr):
+
+    def frame(f, c):
+        lhs = jnp.concatenate([act[f + p].reshape(4 * cj, 3 * ch) for p in range(3)], axis=-1)
+        rhs = jnp.concatenate(
+            [
+                jnp.concatenate([wv[k, r * ch : (r + 1) * ch, :] for r in range(3)], axis=-1)
+                for k in range(9)
+            ],
+            axis=0,
+        )
+        got = jnp.dot(lhs, rhs, preferred_element_type=F32)
         for y in range(2):
-            base = (f * 2 + y) * 2 * cj
-            for b in range(2):
-                value = acc[base + b * cj : base + (b + 1) * cj, :] + b_mid[...]
-                value = value + hid[f + 2, y + 1, b].astype(F32)
+            e0, e1, e2 = [got[2 * y * cj : (2 * y + 1) * cj, r * ch : (r + 1) * ch] for r in range(3)]
+            o0, o1, o2 = [
+                got[(2 * y + 1) * cj : (2 * y + 2) * cj, r * ch : (r + 1) * ch] for r in range(3)
+            ]
+            from_left = jnp.where(edge == 0, 0.0, pltpu.roll(o0, 1, 0))
+            from_right = jnp.where(edge == cj - 1, 0.0, pltpu.roll(e2, cj - 1, 0))
+            for b, value in enumerate((from_left + e1 + o2, e0 + o1 + from_right)):
+                value = value + (hid[f + 2, y + 1, b].astype(F32) + b_mid_c)
                 for piece in range(ch // LANES):
                     cols = slice(piece * LANES, (piece + 1) * LANES)
-                    stage[f * 2 + y, piece, pl.ds(b, cj, 2), :] = value[:, cols]
+                    stage[y, piece, pl.ds(b, cj, 2), :] = value[:, cols]
             for piece in range(ch // LANES):
                 cols = slice(piece * LANES, (piece + 1) * LANES)
-                out[f, y, :, cols] = stage[f * 2 + y, piece].astype(BF16)
+                out[f, y, :, cols] = stage[y, piece].astype(BF16)
+        return c
+
+    lax.fori_loop(0, fr, frame, 0)
 
 
 def body(n_ha, n_ta, latent_tokens, w_in, b_in, gn_gain, gn_shift, w_mid, b_mid):
@@ -287,10 +290,9 @@
     zc = width // 4
     fr, cj, n = frames // n_ta, half * n_ta, n_ha * n_ta
     vm = pl.BlockSpec(memory_space=pltpu.VMEM)
-    row = lambda v: v.reshape(1, ch)
     return pl.pallas_call(
         functools.partial(kernel, n_ha, n_ta),
-        out_shape=jax.ShapeDtypeStruct((fr, 2, 2 * cj, ch), BF16),
+        out_shape=pltpu.VMEM((fr, 2, 2 * cj, ch), BF16),
         in_specs=[vm, vm, vm, vm, vm, pl.BlockSpec(memory_space=pl.ANY), vm],
         out_specs=vm,
         scratch_shapes=[
@@ -299,9 +301,8 @@
             pltpu.VMEM((48 * zc, 4 * ch), BF16),
             pltpu.VMEM((3, frames * cj, 4 * width), BF16),
             pltpu.VMEM((fr + 2, 4, 2, cj, ch), BF16),
-            pltpu.VMEM((fr + 2, 4, 2 * cj, 3 * ch), BF16),
-            pltpu.VMEM((fr * 4 * cj, ch), F32),
-            pltpu.VMEM((fr * 2, ch // LANES, 2 * cj, LANES), F32),
+            pltpu.VMEM((fr + 2, 2, 2 * cj, 3 * ch), BF16),
+            pltpu.VMEM((2, ch // LANES, 2 * cj, LANES), F32),
             pltpu.VMEM((9, 3 * ch, ch), BF16),
             pltpu.VMEM((2, LANES), F32),
             pltpu.VMEM((n, 2, LANES), F32),
@@ -319,8 +320,8 @@
             collective_id=0, has_side_effects=True, vmem_limit_bytes=60 * 1024 * 1024
         ),
     )(
-        latent_tokens, w_in.reshape(9, 3 * zc, ch), row(b_in), row(gn_gain), row(gn_shift),
-        w_mid.reshape(9, 3 * ch, ch), row(b_mid),
+        latent_tokens, w_in.reshape(9, 3 * zc, ch), b_in, gn_gain, gn_shift,
+        w_mid.reshape(9, 3 * ch, ch), b_mid,
     )
 
 

time: 39.7 us -> 28.6 us (0.72)
  local copies, waits for them, and re-layouts: 7.11 us -> 0.88 us
  Pallas kernels: 32.3 us -> 27.6 us
    reshape x4 -> x0, local copies, waits for them, and re-layouts: 5.02 us -> none  [body(): row = lambda v: v.reshape(1, ch)]
    pallas_call x1, Pallas kernels: 32.3 us -> 27.6 us  [body(): pl.pallas_call(functools.partial(kernel, n_ha, n_ta), out_shape=pltpu.VME...]
    unnamed x1, local copies, waits for them, and re-layouts: 2.09 us -> 0.88 us
where the time goes in v2:
time: 28.6 us; the launch traced here: 28.5 us
  Pallas kernels  27.6 us (97%)
  local copies, waits for them, and re-layouts  0.88 us (3%)
    pallas_call x1, Pallas kernels, body(): pl.pallas_call(functools.partial(kernel, n_ha, n_ta), out_shape=pltpu.VME...  27.6 us
    unnamed x1, local copies, waits for them, and re-layouts  0.88 us

profile of v2, /device:TPU:0, one launch (start us, length us, event | category | flops | bytes accessed | tf_op | source)
XLA Modules:
  0.0 28.5 jit_solution(5509391253845905051)
XLA Ops:
  0.0 27.6 %shard_map.73 = bf16[4,2,128,384]{3,2,1,0:T(8,128)(2,1)S(1)} custom-call(bf16[8,32,64]{2,1,0:T(8,128)(2,1)} %tok.1, bf16[9,48,384]{2,1,0:T(8,128)(2,1)} %bitcast.3, f32[384]{0:T(512)} %b_in.1, f32[384]{0:T(512)} %gain.1, f32[384]{0:T(512)} %shift.1, bf16[9,1152,384]{2,1,0:T(8,128)(2,1)} %bitcast.2, f32[384]{0:T(512)} %b_mid.1), custom_call_target="tpu_custom_call" | custom-call | tf_op jit(solution)/shard_map/pallas_call | solution.py:293
  27.6 0.9 %copy.9 = bf16[4,2,128,384]{3,2,1,0:T(8,128)(2,1)} copy(bf16[4,2,128,384]{3,2,1,0:T(8,128)(2,1)S(1)} %shard_map.73) | data formatting | bytes 1572864

commit v3 on v2

--- a/solution.py
+++ b/solution.py
@@ -31,15 +31,15 @@
 
 
 def kernel(
-    n_ha, n_ta, tok, w_in, b_in, gain, shift, w_mid, b_mid, out,
-    pk, rx, wexp, patch, hid, act, stage, wv, stat, gath, sums, spread,
-    w_sem, tx_a, tx_b, rx_a, rx_b, st_tx, st_rx,
+    n_ha, n_ta, tok_hbm, w_in_hbm, b_in, gain, shift, w_mid, b_mid, out,
+    tok, w_in, pk, rx, wexp, patch, hid, act, stage, wv, stat, gath, sums, spread,
+    in_sem, w_sem, tx_a, tx_b, rx_a, rx_b, st_tx, st_rx,
 ):
     h = lax.axis_index("ha")
     t = lax.axis_index("ta")
     n = n_ha * n_ta
     me = h * n_ta + t
-    frames, half, width = tok.shape
+    frames, half, width = tok_hbm.shape
     fr = frames // n_ta
     ch = b_in.shape[-1]
     members = ch // GROUPS
@@ -48,19 +48,12 @@
     ext = fr + 2
     b_in_c, gain_c, shift_c, b_mid_c = [v[...].reshape(1, ch) for v in (b_in, gain, shift, b_mid)]
 
-    for k in range(9):
-        pltpu.make_async_copy(w_mid.at[k], wv.at[k], w_sem.at[k]).start()
-
-    packed = jnp.concatenate([tok[:, : half // 2, :], tok[:, half // 2 :, :]], axis=-1)
-    pk[...] = packed
+    get_tok = pltpu.make_async_copy(tok_hbm, tok, in_sem.at[0])
+    get_w_in = pltpu.make_async_copy(w_in_hbm, w_in, in_sem.at[1])
+    get_tok.start()
     rx[...] = jnp.zeros_like(rx)
-    rx[1, t, pl.ds(fr * (1 - t), fr)] = packed[:fr]
-
-    @pl.when(t == 1)
-    def _():
-        rx[1, 1, fr:] = packed[fr:]
-
     barrier = pltpu.get_barrier_semaphore()
+    together = n - 1 if n <= 16 else 1
 
     def greet(k, c):
         peer = lax.rem(me + k, n)
@@ -69,8 +62,64 @@
         )
         return c
 
-    lax.fori_loop(1, n, greet, 0)
-
+    lax.fori_loop(1, n, greet, 0, unroll=together)
+    get_w_in.start()
+    for k in range(9):
+        pltpu.make_async_copy(w_mid.at[k], wv.at[k], w_sem.at[k]).start()
+
+    chan = lax.broadcasted_iota(jnp.int32, (ch, ch + LANES), 0)
+    lane = lax.broadcasted_iota(jnp.int32, (ch, ch + LANES), 1)
+    target = jnp.where(lane < ch, group_of(lane, members), (lane - ch).astype(F32))
+    sums[...] = jnp.where(group_of(chan, members) == target, 1.0, 0.0).astype(BF16)
+    chan = lax.broadcasted_iota(jnp.int32, (LANES, ch), 1)
+    lane = lax.broadcasted_iota(jnp.int32, (LANES, ch), 0)
+    spread[...] = jnp.where(group_of(chan, members) == lane.astype(F32), 1.0, 0.0).astype(BF16)
+
+    get_tok.wait()
+    packed = jnp.concatenate([tok[:, : half // 2, :], tok[:, half // 2 :, :]], axis=-1)
+    pk[...] = packed
+    rx[1, t, pl.ds(fr * (1 - t), fr)] = packed[:fr]
+
+    @pl.when(t == 1)
+    def _():
+        rx[1, 1, fr:] = packed[fr:]
+
+    pl.semaphore_wait(barrier, n - 1)
+
+    partners = [(0, 1), (1, 0), (-1, 0), (1, 1), (-1, 1)]
+
+    def copies(s):
+        dh, dt = partners[s]
+        other = (t + dt) % n_ta
+        to = {"ha": h + dh, "ta": other}
+        first = pltpu.make_async_remote_copy(
+            src_ref=pk.at[pl.ds(0, fr)],
+            dst_ref=rx.at[1 - dh, t, pl.ds(fr * (1 - other), fr)],
+            send_sem=tx_a.at[s], recv_sem=rx_a.at[s], device_id=to, device_id_type=MESH,
+        )
+        second = pltpu.make_async_remote_copy(
+            src_ref=pk.at[pl.ds(fr, fr)],
+            dst_ref=rx.at[1 - dh, t, pl.ds(fr, fr)],
+            send_sem=tx_b.at[s], recv_sem=rx_b.at[s], device_id=to, device_id_type=MESH,
+        )
+        return first, second, other
+
+    def exists(s, sign):
+        dh = partners[s][0] * sign
+        return jnp.logical_and(h + dh >= 0, h + dh < n_ha)
+
+    for s in range(5):
+
+        @pl.when(exists(s, 1))
+        def _(s=s):
+            first, second, other = copies(s)
+            first.start()
+
+            @pl.when(other == 1)
+            def _():
+                second.start()
+
+    get_w_in.wait()
     zero = jnp.zeros((zc, ch), BF16)
     for p in range(3):
         for block in range(4):
@@ -86,49 +135,6 @@
                             piece = w_in[3 * p + q, r * zc : (r + 1) * zc, :] if inside else zero
                             col = (2 * a + b) * ch
                             wexp[row : row + zc, col : col + ch] = piece
-    chan = lax.broadcasted_iota(jnp.int32, (ch, ch + LANES), 0)
-    lane = lax.broadcasted_iota(jnp.int32, (ch, ch + LANES), 1)
-    target = jnp.where(lane < ch, group_of(lane, members), (lane - ch).astype(F32))
-    sums[...] = jnp.where(group_of(chan, members) == target, 1.0, 0.0).astype(BF16)
-    chan = lax.broadcasted_iota(jnp.int32, (LANES, ch), 1)
-    lane = lax.broadcasted_iota(jnp.int32, (LANES, ch), 0)
-    spread[...] = jnp.where(group_of(chan, members) == lane.astype(F32), 1.0, 0.0).astype(BF16)
-
-    pl.semaphore_wait(barrier, n - 1)
-
-    partners = [(0, 1), (1, 0), (-1, 0), (1, 1), (-1, 1)]
-
-    def copies(s):
-        dh, dt = partners[s]
-        other = (t + dt) % n_ta
-        to = {"ha": h + dh, "ta": other}
-        first = pltpu.make_async_remote_copy(
-            src_ref=pk.at[pl.ds(0, fr)],
-            dst_ref=rx.at[1 - dh, t, pl.ds(fr * (1 - other), fr)],
-            send_sem=tx_a.at[s], recv_sem=rx_a.at[s], device_id=to, device_id_type=MESH,
-        )
-        second = pltpu.make_async_remote_copy(
-            src_ref=pk.at[pl.ds(fr, fr)],
-            dst_ref=rx.at[1 - dh, t, pl.ds(fr, fr)],
-            send_sem=tx_b.at[s], recv_sem=rx_b.at[s], device_id=to, device_id_type=MESH,
-        )
-        return first, second, other
-
-    def exists(s, sign):
-        dh = partners[s][0] * sign
-        return jnp.logical_and(h + dh >= 0, h + dh < n_ha)
-
-    for s in range(5):
-
-        @pl.when(exists(s, 1))
-        def _(s=s):
-            first, second, other = copies(s)
-            first.start()
-
-            @pl.when(other == 1)
-            def _():
-                second.start()
-
     for s in range(5):
 
         @pl.when(exists(s, -1))
@@ -200,7 +206,7 @@
         ).start()
         return c
 
-    lax.fori_loop(1, n, share, 0)
+    lax.fori_loop(1, n, share, 0, unroll=together)
 
     early = conv(1, 0, 2, 0, 4 * ch)
     for ab in range(4):
@@ -290,12 +296,15 @@
     zc = width // 4
     fr, cj, n = frames // n_ta, half * n_ta, n_ha * n_ta
     vm = pl.BlockSpec(memory_space=pltpu.VMEM)
+    far = pl.BlockSpec(memory_space=pl.ANY)
     return pl.pallas_call(
         functools.partial(kernel, n_ha, n_ta),
         out_shape=pltpu.VMEM((fr, 2, 2 * cj, ch), BF16),
-        in_specs=[vm, vm, vm, vm, vm, pl.BlockSpec(memory_space=pl.ANY), vm],
+        in_specs=[far, far, vm, vm, vm, far, vm],
         out_specs=vm,
         scratch_shapes=[
+            pltpu.VMEM((frames, half, width), BF16),
+            pltpu.VMEM((9, 3 * zc, ch), BF16),
             pltpu.VMEM((frames, half // 2, 2 * width), BF16),
             pltpu.VMEM((3, n_ta, frames, half // 2, 2 * width), BF16),
             pltpu.VMEM((48 * zc, 4 * ch), BF16),
@@ -308,6 +317,7 @@
             pltpu.VMEM((n, 2, LANES), F32),
             pltpu.VMEM((ch, ch + LANES), BF16),
             pltpu.VMEM((LANES, ch), BF16),
+            pltpu.SemaphoreType.DMA((2,)),
             pltpu.SemaphoreType.DMA((9,)),
             pltpu.SemaphoreType.DMA((5,)),
             pltpu.SemaphoreType.DMA((5,)),

time: 28.6 us -> 28.5 us (level)
  no operation moved by 1% of the time
where the time goes in v3:
time: 28.5 us; the launch traced here: 28.3 us
  Pallas kernels  27.4 us (96%)
  local copies, waits for them, and re-layouts  0.88 us (3%)
    pallas_call x1, Pallas kernels, body(): pl.pallas_call(functools.partial(kernel, n_ha, n_ta), out_shape=pltpu.VME...  27.4 us
    unnamed x1, local copies, waits for them, and re-layouts  0.88 us

profile of v3, /device:TPU:0, one launch (start us, length us, event | category | flops | bytes accessed | tf_op | source)
XLA Modules:
  0.0 28.3 jit_solution(1395157438439028923)
XLA Ops:
  0.0 27.4 %shard_map.73 = bf16[4,2,128,384]{3,2,1,0:T(8,128)(2,1)S(1)} custom-call(bf16[8,32,64]{2,1,0:T(8,128)(2,1)} %tok_hbm.1, bf16[9,48,384]{2,1,0:T(8,128)(2,1)} %bitcast.3, f32[384]{0:T(512)} %b_in.1, f32[384]{0:T(512)} %gain.1, f32[384]{0:T(512)} %shift.1, bf16[9,1152,384]{2,1,0:T(8,128)(2,1)} %bitcast.2, f32[384]{0:T(512)} %b_mid.1), custom_call_target="tpu_custom_call" | custom-call | tf_op jit(solution)/shard_map/pallas_call | solution.py:300
  27.4 0.9 %copy.9 = bf16[4,2,128,384]{3,2,1,0:T(8,128)(2,1)} copy(bf16[4,2,128,384]{3,2,1,0:T(8,128)(2,1)S(1)} %shard_map.73) | data formatting | bytes 1572864
